TPU v7x, 32 devices: a whole 2x2x4 slice. The times are simulated.
32 devices in a mesh: slab: 16 (over z, x, core), layer: 2 (over y).
Axes of the slice: x: 2, y: 2, z: 4, core: 2. Of those that a mesh axis runs over, the one named last changes fastest.
Arguments:
- nodal_field: float32 [2, 1024, 4, 4, 512], P('layer', 'slab'), may hold values from -6 to 6
- metric: float32 [2, 1024, 4, 4, 3, 512], P('layer', 'slab'), may hold values from 0.25 to 2
- slab_ids: int32 [1024], replicated, may hold values from 0 to 1023, as said below
- face_map: int32 [1024, 1024], P('slab'), may hold values from 0 to 1023, as said below
Outputs:
- assembled: float32 [2, 1024, 4, 4, 512], P('layer', 'slab')
Inputs may be any that keep to these rules, and one draw needn't show every extreme that they name: slab_ids is a permutation of 0 to 1023; positions p of one device are those with p // 64 equal to its index along slab, and for one rotation R every device holds exactly the slabs g with (g + R) mod 16 equal to its index, in any order of its positions, so slab (g + 1) mod 1024 always sits on the next device along slab, cyclically. Each row of face_map is a permutation of 0 to 1023: either the identity, or the map that reverses y, sending (ez, ey, c, b) to (ez, 3 - ey, c, 7 - b); z order is never changed.
All inputs are finite; a program needn't handle non-finite values.
Results may differ from a plain program's by a relative error of at most 0.00005.
Values sent between devices are 32-bit elements; how exact they have to be, the bound alone decides.
A program may use at most 192 MiB of HBM per device.

v0:
```python
import jax
import jax.numpy as jnp
import numpy as np
from jax import lax
from jax.sharding import PartitionSpec as P

P_SIZE = 8
PTS = 512
EY = 4
EZ = 4
FACE = 1024


def from_behind(array, axis, by):
    peers = lax.axis_size(axis)
    return lax.ppermute(array, axis, [(i, (i + by) % peers) for i in range(peers)])


def from_partner(value, axis, apart):
    mask = 2**apart
    pairs = [(source, source ^ mask) for source in range(lax.axis_size(axis))]
    return lax.ppermute(value, axis, pairs)


def legendre_pair(gll_nodes, degree):
    lower_poly = gll_nodes * 0.0 + 1.0
    upper_poly = gll_nodes.copy()
    for poly_order in range(2, degree + 1):
        lower_poly, upper_poly = (
            upper_poly,
            ((2 * poly_order - 1) * gll_nodes * upper_poly - (poly_order - 1) * lower_poly)
            / poly_order,
        )
    return (lower_poly, upper_poly)


def gll_tables():
    degree = P_SIZE - 1
    gll_nodes = -np.cos(np.pi * np.arange(P_SIZE) / degree)
    for newton_sweep in range(100):
        lower_poly, upper_poly = legendre_pair(gll_nodes, degree)
        gll_nodes = gll_nodes - (gll_nodes * upper_poly - lower_poly) / ((degree + 1) * upper_poly)
    lower_poly, upper_poly = legendre_pair(gll_nodes, degree)
    quad_weights = 2.0 / (degree * (degree + 1) * upper_poly * upper_poly)
    identity = np.eye(P_SIZE)
    differ = gll_nodes[:, None] - gll_nodes[None, :] + identity
    derivative = upper_poly[:, None] / (upper_poly[None, :] * differ)
    derivative = derivative * (1.0 - identity)
    derivative[0, 0] = -degree * (degree + 1) / 4.0
    derivative[degree, degree] = degree * (degree + 1) / 4.0
    weight_cube = (
        quad_weights[:, None, None] * quad_weights[None, :, None] * quad_weights[None, None, :]
    )
    identity_two = np.kron(identity, identity)
    along_x = np.kron(identity_two, derivative)
    along_y = np.kron(identity, np.kron(derivative, identity))
    along_z = np.kron(derivative, identity_two)
    operator_stack = np.concatenate([along_x, along_y, along_z], 0)
    weight_rows = np.tile(weight_cube.reshape(-1), 3)
    return (jnp.asarray(operator_stack, jnp.float32), jnp.asarray(weight_rows, jnp.float32))


def local_apply(values, factors, operator_stack, weight_rows):
    highest = lax.Precision.HIGHEST
    gradients = jnp.dot(
        values, operator_stack.T, precision=highest, preferred_element_type=jnp.float32
    )
    fluxes = gradients * (weight_rows * factors)
    result = jnp.dot(fluxes, operator_stack, precision=highest, preferred_element_type=jnp.float32)
    return result.reshape(values.shape[:-1] + (P_SIZE, P_SIZE, P_SIZE))


def assemble_slab(values):
    low_plane = values[..., :, :, :, 0:1, :]
    high_plane = values[..., :, :, :, P_SIZE - 1 : P_SIZE, :]
    zero_plane = jnp.zeros_like(low_plane[..., :, 0:1, :, :, :])
    from_after = jnp.concatenate([low_plane[..., :, 1:, :, :, :], zero_plane], axis=-4)
    from_before = jnp.concatenate([zero_plane, high_plane[..., :, :-1, :, :, :]], axis=-4)
    b_iota = jnp.arange(P_SIZE)[:, None]
    values = (
        values
        + jnp.where(b_iota == P_SIZE - 1, from_after, 0.0)
        + jnp.where(b_iota == 0, from_before, 0.0)
    )
    low_plane = values[..., :, :, 0:1, :, :]
    high_plane = values[..., :, :, P_SIZE - 1 : P_SIZE, :, :]
    zero_plane = jnp.zeros_like(low_plane[..., 0:1, :, :, :, :])
    from_after = jnp.concatenate([low_plane[..., 1:, :, :, :, :], zero_plane], axis=-5)
    from_before = jnp.concatenate([zero_plane, high_plane[..., :-1, :, :, :, :]], axis=-5)
    c_iota = jnp.arange(P_SIZE)[:, None, None]
    values = (
        values
        + jnp.where(c_iota == P_SIZE - 1, from_after, 0.0)
        + jnp.where(c_iota == 0, from_before, 0.0)
    )
    return values


def face_of(local_out, column):
    return local_out[..., column].reshape(local_out.shape[:-5] + (FACE,))


def put_faces(local_out, left_values, right_values):
    inner_shape = local_out.shape[:-1] + (1,)
    return jnp.concatenate(
        [
            left_values.reshape(inner_shape),
            local_out[..., 1 : P_SIZE - 1],
            right_values.reshape(inner_shape),
        ],
        axis=-1,
    )


def flip_face(face_values):
    grid = face_values.reshape(face_values.shape[:-1] + (EZ, EY, P_SIZE, P_SIZE))
    grid = jnp.flip(jnp.flip(grid, -3), -1)
    return grid.reshape(face_values.shape)


def reorient(face_values, flipped):
    return jnp.where(flipped, flip_face(face_values), face_values)


def reorient_edge(edge_values, flipped):
    return jnp.where(flipped, jnp.flip(edge_values, -1), edge_values)


def pick_rows(selector, rows):
    return jnp.einsum("st,...tf->...sf", selector, rows, precision=lax.Precision.HIGHEST)


def body(nodal_field, metric, slab_ids, face_map):
    operator_stack, weight_rows = gll_tables()
    slab_count = nodal_field.shape[1]
    cycle_size = lax.axis_size("slab")
    total_slabs = slab_count * cycle_size
    device = lax.axis_index("slab")
    values = nodal_field.reshape(slab_count, EZ, EY, PTS)
    factors = metric.reshape(slab_count, EZ, EY, 3 * PTS)
    flipped = face_map[:, 0:1] != 0
    local_out = assemble_slab(local_apply(values, factors, operator_stack, weight_rows))
    right_face = face_of(local_out, P_SIZE - 1)
    left_face = face_of(local_out, 0)
    from_prev = from_behind(reorient(right_face, flipped), "slab", 1)
    from_next = from_behind(left_face, "slab", -1)
    own_ids = lax.dynamic_slice_in_dim(slab_ids, device * slab_count, slab_count)
    prev_ids = lax.dynamic_slice_in_dim(
        slab_ids, (device + cycle_size - 1) % cycle_size * slab_count, slab_count
    )
    next_ids = lax.dynamic_slice_in_dim(
        slab_ids, (device + 1) % cycle_size * slab_count, slab_count
    )
    want_prev = (own_ids + total_slabs - 1) % total_slabs
    want_next = (own_ids + 1) % total_slabs
    prev_select = (prev_ids[None, :] == want_prev[:, None]).astype(jnp.float32)
    next_select = (next_ids[None, :] == want_next[:, None]).astype(jnp.float32)
    left_sum = left_face + pick_rows(prev_select, from_prev)
    right_sum = right_face + reorient(pick_rows(next_select, from_next), flipped)
    ez_iota = jnp.arange(EZ)[:, None, None, None, None]
    c_iota = jnp.arange(P_SIZE)[None, None, :, None, None]
    bottom_mask = (ez_iota == 0) & (c_iota == 0)
    top_mask = (ez_iota == EZ - 1) & (c_iota == P_SIZE - 1)
    raw_top = local_out[:, EZ - 1, :, P_SIZE - 1, :, :].reshape(slab_count, EY * P_SIZE * P_SIZE)
    raw_bottom = local_out[:, 0, :, 0, :, :].reshape(slab_count, EY * P_SIZE * P_SIZE)
    partner = from_partner(jnp.stack([raw_bottom, raw_top], 0), "layer", 0)
    edge_grid = partner.reshape(2, slab_count, EY, P_SIZE, P_SIZE)
    far_right = edge_grid[..., P_SIZE - 1].reshape(2, slab_count, EY * P_SIZE)
    far_left = edge_grid[..., 0].reshape(2, slab_count, EY * P_SIZE)
    sent_right = reorient_edge(far_right, flipped[None])
    edges_prev = from_behind(sent_right, "slab", 1)
    edges_next = from_behind(far_left, "slab", -1)
    diag_left = pick_rows(prev_select, edges_prev).reshape(2, slab_count, EY, P_SIZE, 1)
    diag_right = reorient_edge(pick_rows(next_select, edges_next), flipped[None]).reshape(
        2, slab_count, EY, P_SIZE, 1
    )
    middle_zero = jnp.zeros((2, slab_count, EY, P_SIZE, P_SIZE - 2), jnp.float32)
    correction = jnp.concatenate([diag_left, middle_zero, diag_right], axis=-1).reshape(
        2, slab_count, EY * P_SIZE * P_SIZE
    )
    local_out = put_faces(local_out, left_sum, right_sum)
    top_face = local_out[:, EZ - 1, :, P_SIZE - 1, :, :].reshape(slab_count, EY * P_SIZE * P_SIZE)
    bottom_face = local_out[:, 0, :, 0, :, :].reshape(slab_count, EY * P_SIZE * P_SIZE)
    bottom_sum = bottom_face + partner[1] + correction[1]
    top_sum = top_face + partner[0] + correction[0]
    bottom_grid = bottom_sum.reshape(slab_count, 1, EY, 1, P_SIZE, P_SIZE)
    top_grid = top_sum.reshape(slab_count, 1, EY, 1, P_SIZE, P_SIZE)
    local_out = jnp.where(bottom_mask, bottom_grid, local_out)
    local_out = jnp.where(top_mask, top_grid, local_out)
    return local_out.reshape(1, slab_count, EZ, EY, PTS)


def solution(mesh):
    return jax.shard_map(
        body,
        mesh=mesh,
        in_specs=(
            P("layer", "slab", None, None, None),
            P("layer", "slab", None, None, None, None),
            P(),
            P("slab", None),
        ),
        out_specs=P("layer", "slab", None, None, None),
        check_vma=False,
    )
```

profile of v0, /device:TPU:0, one launch (start us, length us, event | category | flops | bytes accessed | tf_op | source)
XLA Modules:
  0.0 100.0 jit_solution(5411365979549020003)
XLA Ops:
  0.0 9.4 %copy.18 = f32[1,64,4,4,3,512]{5,4,1,3,2,0:T(4,128)} copy(f32[1,64,4,4,3,512]{5,3,4,2,1,0:T(4,128)} %param.7) | data formatting | bytes 12582912 | tf_op args[1]
  9.4 11.4 %reshape.145 = f32[64,4,4,1536]{3,0,2,1:T(8,128)} reshape(f32[1,64,4,4,3,512]{5,4,1,3,2,0:T(4,128)} %copy.18) | data formatting | bytes 12582912 | tf_op jit(solution)/shard_map/reshape | solution.py:140
  20.8 13.5 %fusion.3 = f32[1536,64,4,4]{0,1,3,2:T(8,128)S(1)} fusion(f32[1536,512,1,1]{1,0,3,2:T(8,128)} %constant.85, f32[64,4,4,512]{3,2,1,0:T(4,128)S(1)} %bitcast.90), kind=kOutput, calls=%fused_computation.8 | convolution fusion | flops 9663676416 | bytes 11534336 | tf_op jit(solution)/shard_map/dot_general | solution.py:65
  34.4 21.0 %fusion = f32[64,4,4,512]{0,3,2,1:T(8,128)S(1)} fusion(f32[1536,512,1,1]{1,0,3,2:T(8,128)S(1)} %copy-done.4, f32[1536,64,4,4]{0,1,3,2:T(8,128)S(1)} %fusion.3, f32[64,4,4,1536]{3,0,2,1:T(8,128)S(1)} %copy-done.3, f32[1536]{0:T(1024)S(1)} %copy-done.5), kind=kOutput, calls=%fused_computation.1 | convolution fusion | flops 9666822144 | bytes 17831936 | tf_op jit(solution)/shard_map/dot_general | solution.py:69
  55.4 0.1 fusion.28
  55.5 0.1 pad_bitcast_fusion.2
  55.6 1.3 %select_add_fusion.1 = f32[64,4,4,8,8,8]{0,5,4,3,2,1:T(8,128)S(1)} fusion(f32[64,4,4,8,8,8]{0,5,4,3,2,1:T(8,128)S(1)} %bitcast.92, f32[64,4,4,8,8]{0,4,3,2,1:T(8,128)S(1)} %get-tuple-element.25, f32[64,4,4,8,8]{0,4,3,2,1:T(8,128)S(1)} %get-tuple-element.26, pred[8]{0:T(512)(128)(4,1)S(1)} %get-tuple-element.27, pred[8]{0:T(512)(128)(4,1)S(1)} %get-tuple-element.28), kind=kLoop, calls=%fused_computation.6 | loop fusion | flops 2097152 | bytes 4718608 | tf_op jit(solution)/shard_map/add | solution.py:81
  56.9 0.1 fusion.27
  57.0 1.6 %select_add_fusion = f32[64,4,4,8,8,8]{0,5,4,3,2,1:T(8,128)S(1)} fusion(f32[64,4,4,8,8]{0,4,3,2,1:T(8,128)S(1)} %pad_bitcast_fusion, f32[64,4,4,8,8]{0,4,3,2,1:T(8,128)S(1)} %pad_bitcast_fusion.1, pred[8]{0:T(512)(128)(4,1)S(1)} %get-tuple-element.27, pred[8]{0:T(512)(128)(4,1)S(1)} %get-tuple-element.28, f32[64,4,4,8,8]{0,4,3,2,1:T(8,128)S(1)} %get-tuple-element.25, ...), kind=kLoop, calls=%fused_computation.5 | loop fusion | flops 4194304 | bytes 5242896 | tf_op jit(solution)/shard_map/add | solution.py:92
  58.7 3.1 %collective-permute-start.2 = (f32[2,64,256]{1,2,0:T(8,128)S(1)}, f32[2,64,256]{1,2,0:T(8,128)S(1)}, u32[]{:S(2)}, u32[]{:S(2)}) collective-permute-start(f32[2,64,256]{1,2,0:T(8,128)S(1)} %pad_maximum_fusion.1), channel_id=1, source_target_pairs={{0,1},{1,0},{2,3},{3,2},{4,5},{5,4},{6,7},{7,6},{8,9},{9,8},{10,11... | collective-permute-start | bytes 393224 | tf_op jit(solution)/shard_map/ppermute | solution.py:22
  61.8 1.0 %fusion.26 = (f32[64,4,4,8,8,1]{0,5,4,3,2,1:T(1,128)S(1)}, f32[64,4,4,8,8,1]{0,5,4,3,2,1:T(1,128)S(1)}) fusion(f32[64,4,4,8,8,8]{0,5,4,3,2,1:T(8,128)S(1)} %select_add_fusion), kind=kLoop, calls=%fused_computation.62 | loop fusion | bytes 1048576 | tf_op jit(solution)/shard_map/slice | solution.py:100
  62.8 4.3 %collective-permute-start.1 = (f32[64,1024]{0,1:T(8,128)S(1)}, f32[64,1024]{0,1:T(8,128)S(1)}, u32[]{:S(2)}, u32[]{:S(2)}) collective-permute-start(f32[64,1024]{0,1:T(8,128)S(1)} %bitcast.104), channel_id=1, source_target_pairs={{0,30},{2,0},{4,2},{6,4},{8,6},{10,8},{12,10},{14,12},{16,14},{18,... | collective-permute-start | bytes 786440 | tf_op jit(solution)/shard_map/ppermute | solution.py:16
  67.1 0.1 broadcast_and_fusion.1
  67.2 0.1 broadcast_and_fusion
  67.3 0.9 and_select_fusion.1
  68.1 0.2 copy.22
  68.3 5.1 %slice.88 = f32[64,4,4,8,8,6]{0,5,4,3,2,1:T(8,128)} slice(f32[64,4,4,8,8,8]{0,5,4,3,2,1:T(8,128)} %copy-done.2), slice={[0:64], [0:4], [0:4], [0:8], [0:8], [1:7]} | slice | bytes 3145728 | tf_op jit(solution)/shard_map/slice | solution.py:108
  73.5 0.1 rev.17
  73.5 0.2 copy.20
  73.7 0.2 copy.21
  73.9 0.1 broadcast_in_dim.154
  74.0 0.1 broadcast_in_dim.155
  74.1 0.1 broadcast_in_dim.178
  74.3 0.1 broadcast_in_dim.179
  74.4 0.1 pad.5.clone
  74.5 0.9 fusion.14
  75.4 0.7 collective-permute-start.4
  76.2 1.6 %collective-permute-done.4 = f32[2,64,32]{1,2,0:T(8,128)S(1)} collective-permute-done((f32[2,64,32]{1,2,0:T(8,128)S(1)}, f32[2,64,32]{1,2,0:T(8,128)S(1)}, u32[]{:S(2)}, u32[]{:S(2)}) %collective-permute-start.4) | collective-permute-done | bytes 16416 | tf_op jit(solution)/shard_map/ppermute | solution.py:16
  77.7 0.2 convolution_bitcast_fusion
  78.0 0.1 collective-permute-start.3
  78.1 0.5 fusion.10
  78.5 0.2 copy.24
  78.7 0.1 rev.18
  78.8 0.2 copy.25
  79.0 0.1 broadcast_select_fusion
  79.1 0.1 collective-permute-start
  79.2 4.9 %collective-permute-done.3 = f32[2,64,32]{1,2,0:T(8,128)S(1)} collective-permute-done((f32[2,64,32]{1,2,0:T(8,128)S(1)}, f32[2,64,32]{1,2,0:T(8,128)S(1)}, u32[]{:S(2)}, u32[]{:S(2)}) %collective-permute-start.3) | collective-permute-done | bytes 16416 | tf_op jit(solution)/shard_map/ppermute | solution.py:16
  84.1 0.2 fusion.13
  84.3 0.1 pad_maximum_fusion.2
  84.4 0.2 copy.27
  84.6 3.0 %collective-permute-done = f32[64,1024]{1,0:T(8,128)S(1)} collective-permute-done((f32[64,1024]{1,0:T(8,128)S(1)}, f32[64,1024]{1,0:T(8,128)S(1)}, u32[]{:S(2)}, u32[]{:S(2)}) %collective-permute-start) | collective-permute-done | bytes 262176 | tf_op jit(solution)/shard_map/ppermute | solution.py:16
  87.7 0.3 convolution_add_fusion
  88.0 0.2 copy.23
  88.2 3.8 %pad_maximum_fusion = f32[64,4,4,8,8,8]{0,5,4,3,2,1:T(8,128)S(1)} fusion(f32[64,4,4,8,8,1]{0,5,4,3,2,1:T(1,128)S(1)} %bitcast.99, f32[64,4,4,8,8,6]{0,5,4,3,2,1:T(8,128)} %slice.88, f32[64,4,4,8,8,1]{0,5,4,3,2,1:T(1,128)S(1)} %bitcast.100), kind=kLoop, calls=%fused_computation.3 | loop fusion | flops 1048576 | bytes 4194304 | tf_op jit(solution)/shard_map/concatenate | solution.py:105
  92.1 0.1 broadcast_in_dim.175
  92.2 0.1 broadcast_in_dim.182
  92.4 2.8 %select_select_fusion = f32[1,64,4,4,512]{1,4,3,2,0:T(8,128)} fusion(f32[1,64,4,4,512]{1,4,3,2,0:T(8,128)S(1)} %bitcast.94, f32[64,4,512]{0,2,1:T(8,128)S(1)} %bitcast.98, f32[64,4,512]{0,2,1:T(8,128)S(1)} %bitcast.97, pred[4,512]{1,0:T(4,128)(4,1)S(1)} %broadcast_in_dim.179, pred[4,512]{1,0:T(4,128)(4,1)S(1)} %broadcast_in_dim.155), kind=kLoop, calls=%fused_computation.4 | loop fusion | flops 1048576 | bytes 5246976 | tf_op jit(solution)/shard_map/jit(_where)/select_n | solution.py:189
  95.1 4.8 %copy.34 = f32[1,64,4,4,512]{4,3,2,1,0:T(4,128)} copy(f32[1,64,4,4,512]{1,4,3,2,0:T(8,128)} %select_select_fusion) | data formatting | bytes 4194304 | tf_op jit(solution)/shard_map/jit(_where)/select_n | solution.py:189
  (29 shorter events, 0.3 us)
Async XLA Ops:
  0.0 20.8 %copy-start = (f32[1,64,4,4,512]{4,3,2,1,0:T(4,128)S(1)}, f32[1,64,4,4,512]{4,3,2,1,0:T(4,128)}, u32[]{:S(2)}) copy-start(f32[1,64,4,4,512]{4,3,2,1,0:T(4,128)} %param.6) | copy-start | bytes 6291460
  20.8 13.6 %copy-start.3 = (f32[64,4,4,1536]{3,0,2,1:T(8,128)S(1)}, f32[64,4,4,1536]{3,0,2,1:T(8,128)}, u32[]{:S(2)}) copy-start(f32[64,4,4,1536]{3,0,2,1:T(8,128)} %reshape.145) | copy-start | bytes 18874372
  20.8 13.6 %copy-start.4 = (f32[1536,512,1,1]{1,0,3,2:T(8,128)S(1)}, f32[1536,512,1,1]{1,0,3,2:T(8,128)}, u32[]{:S(2)}) copy-start(f32[1536,512,1,1]{1,0,3,2:T(8,128)} %constant.85) | copy-start | bytes 9437188
  20.8 13.6 %copy-start.5 = (f32[1536]{0:T(1024)S(1)}, f32[1536]{0:T(1024)}, u32[]{:S(2)}) copy-start(f32[1536]{0:T(1024)} %constant.74.clone) | copy-start | bytes 18436
  58.6 3.1 %copy-start.2 = (f32[64,4,4,8,8,8]{0,5,4,3,2,1:T(8,128)}, f32[64,4,4,8,8,8]{0,5,4,3,2,1:T(8,128)S(1)}, u32[]{:S(2)}) copy-start(f32[64,4,4,8,8,8]{0,5,4,3,2,1:T(8,128)S(1)} %select_add_fusion) | copy-start | bytes 6291460
  58.7 16.7 %collective-permute-start.2 = (f32[2,64,256]{1,2,0:T(8,128)S(1)}, f32[2,64,256]{1,2,0:T(8,128)S(1)}, u32[]{:S(2)}, u32[]{:S(2)}) collective-permute-start(f32[2,64,256]{1,2,0:T(8,128)S(1)} %pad_maximum_fusion.1), channel_id=1, source_target_pairs={{0,1},{1,0},{2,3},{3,2},{4,5},{5,4},{6,7},{7,6},{8,9},{9,8},{10,11... | collective-permute-start | bytes 393224 | tf_op jit(solution)/shard_map/ppermute | solution.py:22
  62.8 15.3 %collective-permute-start.1 = (f32[64,1024]{0,1:T(8,128)S(1)}, f32[64,1024]{0,1:T(8,128)S(1)}, u32[]{:S(2)}, u32[]{:S(2)}) collective-permute-start(f32[64,1024]{0,1:T(8,128)S(1)} %bitcast.104), channel_id=1, source_target_pairs={{0,30},{2,0},{4,2},{6,4},{8,6},{10,8},{12,10},{14,12},{16,14},{18,... | collective-permute-start | bytes 786440 | tf_op jit(solution)/shard_map/ppermute | solution.py:16
  75.4 2.3 %collective-permute-start.4 = (f32[2,64,32]{1,2,0:T(8,128)S(1)}, f32[2,64,32]{1,2,0:T(8,128)S(1)}, u32[]{:S(2)}, u32[]{:S(2)}) collective-permute-start(f32[2,64,32]{1,2,0:T(8,128)S(1)} %bitcast.115), channel_id=1, source_target_pairs={{0,30},{2,0},{4,2},{6,4},{8,6},{10,8},{12,10},{14,12},{16,14},{18,... | collective-permute-start | bytes 49160 | tf_op jit(solution)/shard_map/ppermute | solution.py:16
  78.0 6.1 %collective-permute-start.3 = (f32[2,64,32]{1,2,0:T(8,128)S(1)}, f32[2,64,32]{1,2,0:T(8,128)S(1)}, u32[]{:S(2)}, u32[]{:S(2)}) collective-permute-start(f32[2,64,32]{1,2,0:T(8,128)S(1)} %get-tuple-element.23), channel_id=1, source_target_pairs={{0,2},{2,4},{4,6},{6,8},{8,10},{10,12},{12,14},{14,16},{16,18},{18... | collective-permute-start | bytes 49160 | tf_op jit(solution)/shard_map/ppermute | solution.py:16
  79.1 8.5 %collective-permute-start = (f32[64,1024]{1,0:T(8,128)S(1)}, f32[64,1024]{1,0:T(8,128)S(1)}, u32[]{:S(2)}, u32[]{:S(2)}) collective-permute-start(f32[64,1024]{1,0:T(8,128)S(1)} %get-tuple-element.13), channel_id=1, source_target_pairs={{0,2},{2,4},{4,6},{6,8},{8,10},{10,12},{12,14},{14,16},{16,18},{18... | collective-permute-start | bytes 786440 | tf_op jit(solution)/shard_map/ppermute | solution.py:16
  92.3 7.6 %copy-start.1 = (f32[1,64,4,4,512]{4,3,2,1,0:T(4,128)S(1)}, f32[1,64,4,4,512]{4,3,2,1,0:T(4,128)}, u32[]{:S(2)}) copy-start(f32[1,64,4,4,512]{4,3,2,1,0:T(4,128)} %param.6) | copy-start | bytes 6291460
where the time goes:
time: 101 us; the launch traced here: 100 us
  matrix products  35.7 us (35%)
  local copies, waits for them, and re-layouts  34.4 us (34%)
  other arithmetic  11.7 us (12%)
  waiting for transfers between devices  9.51 us (9%)
  starting transfers between devices  8.23 us (8%)
    dot_general x1, matrix products, local_apply(): jnp.dot(fluxes, operator_stack, precision=highest, preferred_element_type...  21 us
    dot_general x1, matrix products, local_apply(): jnp.dot(values, operator_stack.T, precision=highest, preferred_element_ty...  13.5 us
    reshape x1, local copies, waits for them, and re-layouts, body(): factors = metric.reshape(slab_count, EZ, EY, 3 * PTS)  11.4 us
    ppermute x4, waiting for transfers between devices, from_behind(): lax.ppermute(array, axis, [(i, (i + by) % peers) for i in range(peers)])  9.51 us
    unnamed x13, local copies, waits for them, and re-layouts  9.43 us
    ppermute x4, starting transfers between devices, from_behind(): lax.ppermute(array, axis, [(i, (i + by) % peers) for i in range(peers)])  5.17 us
    slice x1, local copies, waits for them, and re-layouts, put_faces(): local_out[..., 1:P_SIZE - 1]  5.13 us
    select_n x1, local copies, waits for them, and re-layouts, body(): local_out = jnp.where(top_mask, top_grid, local_out)  4.8 us
  transfers between devices with their start and end apart: 5, of which 3 were waited for; matrix products, arithmetic and copies ran while one was open for 11% of the time, Pallas kernels for 0%

commit v1 on v0

v1 whole, which is shorter than its diff:
```python
import functools

import jax
import jax.numpy as jnp
import numpy as np
from jax import lax
from jax.experimental import pallas as pl
from jax.experimental.pallas import tpu as pltpu
from jax.sharding import PartitionSpec as P

P_SIZE = 8
PTS = 512
EY = 4
EZ = 4
SUB = 8
LANES = 128


def legendre_pair(nodes, degree):
    lower = nodes * 0.0 + 1.0
    upper = nodes.copy()
    for order in range(2, degree + 1):
        lower, upper = upper, ((2 * order - 1) * nodes * upper - (order - 1) * lower) / order
    return lower, upper


def gll_tables():
    degree = P_SIZE - 1
    nodes = -np.cos(np.pi * np.arange(P_SIZE) / degree)
    for _ in range(100):
        lower, upper = legendre_pair(nodes, degree)
        nodes = nodes - (nodes * upper - lower) / ((degree + 1) * upper)
    lower, upper = legendre_pair(nodes, degree)
    rho = 2.0 / (degree * (degree + 1) * upper * upper)
    eye = np.eye(P_SIZE)
    differ = nodes[:, None] - nodes[None, :] + eye
    der = upper[:, None] / (upper[None, :] * differ) * (1.0 - eye)
    der[0, 0] = -degree * (degree + 1) / 4.0
    der[degree, degree] = degree * (degree + 1) / 4.0
    return der, rho


def two_parts(table):
    high = np.asarray(table, np.float32).astype(jnp.bfloat16)
    low = (table - high.astype(np.float64)).astype(jnp.bfloat16)
    return high, low


def tables():
    der, rho = gll_tables()
    eye8, eye2 = np.eye(8), np.eye(2)
    plane = np.tile(np.kron(rho, rho), 2)
    fwd = np.concatenate(
        [np.kron(np.eye(16), der.T) * plane, np.kron(eye2, np.kron(der.T, eye8)) * plane], 1
    )
    high, low = two_parts(fwd)
    fwd_op = np.concatenate([high, high, low], 0)
    bwd = np.concatenate([np.kron(np.eye(16), der), np.kron(eye2, np.kron(der, eye8))], 0)
    high, low = two_parts(bwd)
    half = np.concatenate([high, low], 1)
    bwd_op = np.concatenate([half, half], 0)
    l2 = (np.arange(SUB) // EY)[:, None]
    h = (np.arange(LANES) // 64)[None, :]
    cube_plane = plane[None, :]
    zf = np.zeros((2, 2, 2, 2, SUB, LANES))
    zb = np.zeros((2, 2, 2, 2, SUB, LANES))
    rc = np.zeros((2, SUB, LANES))
    for lo in range(2):
        c_out = 2 * (2 * lo + l2) + h
        rc[lo] = rho[c_out]
        for li in range(2):
            for s in range(2):
                for l in range(2):
                    c_in = 2 * (2 * li + (l2 ^ s)) + (h ^ l)
                    zf[lo, li, s, l] = der[c_out, c_in] * rho[c_out] * cube_plane
                    zb[lo, li, s, l] = der[c_in, c_out]
    consts = np.concatenate([zf.reshape(-1, SUB, LANES), zb.reshape(-1, SUB, LANES), rc], 0)
    return fwd_op, bwd_op, consts.astype(np.float32)


def roll_sub(x, by):
    return pltpu.roll(x, by % SUB, axis=x.ndim - 2)


def roll_lane(x, by):
    return pltpu.roll(x, by % LANES, axis=x.ndim - 1)


def split(x):
    high = x.astype(jnp.bfloat16)
    return high, (x - high.astype(jnp.float32)).astype(jnp.bfloat16)


def iotas():
    sub = lax.broadcasted_iota(jnp.int32, (SUB, LANES), 0)
    lane = lax.broadcasted_iota(jnp.int32, (SUB, LANES), 1)
    return sub, lane


def lane_gather(x, index):
    return jnp.take_along_axis(x, index, axis=1, mode="promise_in_bounds")


def flip(x, sub, lane):
    y = lane_gather(x, lane ^ 7)
    e = sub % EY
    return jnp.where(
        e == 0, roll_sub(y, -3), jnp.where(e == 1, roll_sub(y, -1), jnp.where(e == 2, roll_sub(y, 1), roll_sub(y, 3)))
    )


def apply_z(pair, consts, base):
    terms = []
    for v in pair:
        sv = roll_sub(v, 4)
        terms += [v, roll_lane(v, 64), sv, roll_lane(sv, 64)]
    out = []
    for lo in range(2):
        acc = consts[base + 8 * lo] * terms[0]
        for t in range(1, 8):
            acc = acc + consts[base + 8 * lo + t] * terms[t]
        out.append(acc)
    return out


def slab_work(sb, u_ref, m_ref, fm_ref, fwd_ref, bwd_ref, consts, put_v, put_faces):
    rows = sb * 64
    u = u_ref[...]
    high, low = split(u)
    g = jnp.dot(
        jnp.concatenate([high, low, high], 1), fwd_ref[...], preferred_element_type=jnp.float32
    )
    m = m_ref[...].reshape(sb * EZ, 3, 16, LANES)
    gx = g[:, :LANES].reshape(sb * EZ, 16, LANES)
    gy = g[:, LANES:].reshape(sb * EZ, 16, LANES)
    fx = (gx * m[:, 0]).reshape(rows, LANES)
    fy = (gy * m[:, 1]).reshape(rows, LANES)
    xh, xl = split(fx)
    yh, yl = split(fy)
    r = jnp.dot(
        jnp.concatenate([xh, yh, xl, yl], 1), bwd_ref[...], preferred_element_type=jnp.float32
    )
    r = (r[:, :LANES] + r[:, LANES:]).reshape(sb * EZ, 2, SUB, LANES)
    u4 = u.reshape(sb * EZ, 2, SUB, LANES)
    mz = m[:, 2].reshape(sb * EZ, 2, SUB, LANES)
    sub, lane = iotas()
    ey, b = sub % EY, lane // 8 % 8
    mask_up = (ey < EY - 1) & (b == 7)
    mask_dn = (ey > 0) & (b == 0)
    top_mask = (sub >= 4) & (lane >= 64)
    bot_mask = (sub < 4) & (lane < 64)
    group = lane // 16
    pick = (lane % 16) * 8
    edges = [None, None]
    z_hold = None
    for s in range(sb):
        v = []
        for ez in range(EZ):
            i = s * EZ + ez
            gz = apply_z([u4[i, 0], u4[i, 1]], consts, 0)
            out = apply_z([gz[0] * mz[i, 0], gz[1] * mz[i, 1]], consts, 16)
            for t in range(2):
                w = out[t] + consts[32 + t] * r[i, t]
                up = roll_lane(roll_sub(w, -1), 56)
                dn = roll_lane(roll_sub(w, 1), -56)
                v.append(w + jnp.where(mask_up, up, 0.0) + jnp.where(mask_dn, dn, 0.0))
        for ez in range(EZ - 1):
            a, c = v[2 * ez + 1], v[2 * ez + 2]
            v[2 * ez + 1] = a + jnp.where(top_mask, roll_lane(roll_sub(c, 4), 64), 0.0)
            v[2 * ez + 2] = c + jnp.where(bot_mask, roll_lane(roll_sub(a, 4), 64), 0.0)
        left = jnp.zeros((SUB, LANES), jnp.float32)
        right = left
        for k in range(8):
            put_v(s, k, v[k])
            left = jnp.where(group == k, lane_gather(v[k], pick), left)
            right = jnp.where(group == k, lane_gather(v[k], pick + 7), right)
        flag = jnp.broadcast_to(fm_ref[s : s + 1, 0:1], (SUB, LANES)) != 0
        right = jnp.where(flag, flip(right, sub, lane), right)
        put_faces(0, s, right)
        put_faces(1, s, left)
        for side, face in enumerate((right, left)):
            edge = roll_sub(jnp.where(sub < 4, face, roll_lane(face, 8)), 4)
            edge = roll_lane(edge, 8 * s) if s else edge
            edges[side] = edge if s == 0 else jnp.where(lane // 8 == s, edge, edges[side])
        z = jnp.where(sub < 4, v[0], v[7])
        if s % 2 == 0:
            z_hold = z
        else:
            put_faces(2, s // 2, jnp.where((sub < 4) == (lane < 64), z_hold, roll_lane(z, 64)))
    put_faces(3, 0, edges[0])
    put_faces(4, 0, edges[1])


def local_kernel(sb, u_ref, m_ref, fm_ref, fwd_ref, bwd_ref, consts, v_ref, pr_ref, pl_ref, z_ref, er_ref, el_ref):
    faces = (pr_ref, pl_ref, z_ref, er_ref, el_ref)

    def put_v(s, k, value):
        v_ref[pl.ds(s * 64 + k * 8, 8), :] = value

    def put_faces(which, at, value):
        faces[which][at] = value

    slab_work(sb, u_ref, m_ref, fm_ref, fwd_ref, bwd_ref, consts, put_v, put_faces)


def finish_kernel(
    sb, slabs, peers, ids_ref, v_ref, fm_ref, pr_ref, pl_ref, z_ref, er_ref, el_ref, out_ref, inv_ref
):
    step = pl.program_id(0)
    me = lax.axis_index("slab")
    total = slabs * peers
    behind = lax.rem(me + peers - 1, peers) * slabs
    ahead = lax.rem(me + 1, peers) * slabs

    @pl.when(step == 0)
    def _():
        for p in range(slabs):
            inv_ref[0, ids_ref[behind + p] // peers] = p
            inv_ref[1, ids_ref[ahead + p] // peers] = p

    sub, lane = iotas()
    top_mask = (sub >= 4) & (lane >= 64)
    bot_mask = (sub < 4) & (lane < 64)
    a = lane % 8
    spread = lane // 8

    def edge_of(ref, q):
        e = pltpu.roll(ref[q // sb], (LANES - 8 * (q % sb)) % LANES, axis=1)
        return jnp.where(
            (sub < 4) & (lane < 8), e, jnp.where((sub >= 4) & (lane >= 120), roll_lane(e, -8), 0.0)
        )

    for s in range(sb):
        own = ids_ref[me * slabs + step * sb + s]
        q_prev = inv_ref[0, lax.rem(own + total - 1, total) // peers]
        q_next = inv_ref[1, lax.rem(own + 1, total) // peers]
        left = pr_ref[q_prev] + edge_of(er_ref, q_prev)
        right = pl_ref[q_next] + edge_of(el_ref, q_next)
        flag = jnp.broadcast_to(fm_ref[s : s + 1, 0:1], (SUB, LANES)) != 0
        right = jnp.where(flag, flip(right, sub, lane), right)
        z = z_ref[s // 2]
        if s % 2:
            z = roll_lane(z, 64)
        z = roll_lane(roll_sub(z, 4), 64)
        for k in range(8):
            add = jnp.where(
                a == 0,
                lane_gather(left, spread + 16 * k),
                jnp.where(a == 7, lane_gather(right, spread + 16 * k), 0.0),
            )
            w = v_ref[pl.ds(s * 64 + k * 8, 8), :] + add
            if k == 0:
                w = w + jnp.where(bot_mask, z, 0.0)
            if k == 7:
                w = w + jnp.where(top_mask, z, 0.0)
            out_ref[pl.ds(s * 64 + k * 8, 8), :] = w


def body(sb, peers, nodal_field, metric, slab_ids, face_map):
    slabs = nodal_field.shape[1]
    steps = slabs // sb
    fwd_op, bwd_op, consts = tables()
    u = nodal_field.reshape(slabs, EZ, EY, 4, LANES).transpose(0, 1, 3, 2, 4).reshape(slabs * 64, LANES)
    m = (
        metric.reshape(slabs, EZ, EY, 3, 4, LANES)
        .transpose(0, 1, 3, 4, 2, 5)
        .reshape(slabs * 192, LANES)
    )
    f32 = jnp.float32
    whole = lambda shape: pl.BlockSpec(shape, lambda i: (0,) * len(shape))
    stack = lambda n: pl.BlockSpec((n, SUB, LANES), lambda i: (i, 0, 0))
    v, pr, plf, z, er, el = pl.pallas_call(
        functools.partial(local_kernel, sb),
        grid=(steps,),
        in_specs=[
            pl.BlockSpec((sb * 64, LANES), lambda i: (i, 0)),
            pl.BlockSpec((sb * 192, LANES), lambda i: (i, 0)),
            pl.BlockSpec((sb, LANES), lambda i: (i, 0)),
            whole(fwd_op.shape),
            whole(bwd_op.shape),
            whole(consts.shape),
        ],
        out_specs=[
            pl.BlockSpec((sb * 64, LANES), lambda i: (i, 0)),
            stack(sb),
            stack(sb),
            stack(sb // 2),
            stack(1),
            stack(1),
        ],
        out_shape=[
            jax.ShapeDtypeStruct((slabs * 64, LANES), f32),
            jax.ShapeDtypeStruct((slabs, SUB, LANES), f32),
            jax.ShapeDtypeStruct((slabs, SUB, LANES), f32),
            jax.ShapeDtypeStruct((slabs // 2, SUB, LANES), f32),
            jax.ShapeDtypeStruct((steps, SUB, LANES), f32),
            jax.ShapeDtypeStruct((steps, SUB, LANES), f32),
        ],
        name="local",
    )(u, m, face_map, jnp.asarray(fwd_op), jnp.asarray(bwd_op), jnp.asarray(consts))
    ring = [(i, (i + 1) % peers) for i in range(peers)]
    back = [(j, i) for i, j in ring]
    both = lambda pairs: [(2 * i + l, 2 * j + 1 - l) for i, j in pairs for l in range(2)]
    pr = lax.ppermute(pr, "slab", ring)
    plf = lax.ppermute(plf, "slab", back)
    z = lax.ppermute(z, "layer", [(0, 1), (1, 0)])
    er = lax.ppermute(er, ("slab", "layer"), both(ring))
    el = lax.ppermute(el, ("slab", "layer"), both(back))
    out = pl.pallas_call(
        functools.partial(finish_kernel, sb, slabs, peers),
        grid=(steps,),
        in_specs=[
            pl.BlockSpec(memory_space=pltpu.SMEM),
            pl.BlockSpec((sb * 64, LANES), lambda i: (i, 0)),
            pl.BlockSpec((sb, LANES), lambda i: (i, 0)),
            whole((slabs, SUB, LANES)),
            whole((slabs, SUB, LANES)),
            stack(sb // 2),
            whole((steps, SUB, LANES)),
            whole((steps, SUB, LANES)),
        ],
        out_specs=pl.BlockSpec((sb * 64, LANES), lambda i: (i, 0)),
        out_shape=jax.ShapeDtypeStruct((slabs * 64, LANES), f32),
        scratch_shapes=[pltpu.SMEM((2, slabs), jnp.int32)],
        name="finish",
    )(slab_ids, v, face_map, pr, plf, z, er, el)
    out = out.reshape(slabs, EZ, 4, EY, LANES).transpose(0, 1, 3, 2, 4)
    return out.reshape(1, slabs, EZ, EY, PTS)


def solution(mesh):
    return jax.shard_map(
        functools.partial(body, 8, mesh.shape["slab"]),
        mesh=mesh,
        in_specs=(
            P("layer", "slab", None, None, None),
            P("layer", "slab", None, None, None, None),
            P(),
            P("slab", None),
        ),
        out_specs=P("layer", "slab", None, None, None),
        check_vma=False,
    )
```

time: 101 us -> 42.9 us (0.42)
  matrix products: 35.7 us -> 0 us
  local copies, waits for them, and re-layouts: 34.4 us -> 0.83 us
  Pallas kernels: 0 us -> 26.9 us
  other arithmetic: 11.7 us -> 0 us
  waiting for transfers between devices: 9.51 us -> 1.92 us
  starting transfers between devices: 8.23 us -> 12.8 us
    dot_general x6 -> x0, matrix products: 35.7 us -> none  [the longest x1 21 us: local_apply(): jnp.dot(fluxes, operator_stack, precision=highest, preferred_element_type...]
    pallas_call x0 -> x2, Pallas kernels: none -> 26.9 us  [the longest x1 17 us: body(): pl.pallas_call(functools.partial(local_kernel, sb), grid=(steps,), in_spe...]
    reshape x3 -> x0, local copies, waits for them, and re-layouts: 11.8 us -> none  [the longest x1 11.4 us: body(): factors = metric.reshape(slab_count, EZ, EY, 3 * PTS)]
    unnamed x13 -> x10, local copies, waits for them, and re-layouts: 9.43 us -> 0.83 us
    ppermute x5, waiting for transfers between devices: 9.51 us -> 1.92 us  [the longest x1 1.8 us: body(): er = lax.ppermute(er, ('slab', 'layer'), both(ring))]
    slice x7 -> x0, local copies, waits for them, and re-layouts: 6.36 us -> none  [the longest x1 5.13 us: put_faces(): local_out[..., 1:P_SIZE - 1]]
    select_n x1 -> x0, local copies, waits for them, and re-layouts: 4.8 us -> none  [body(): local_out = jnp.where(top_mask, top_grid, local_out)]
    ppermute x5, starting transfers between devices: 8.23 us -> 12.8 us  [the longest x1 5.34 us: body(): el = lax.ppermute(el, ('slab', 'layer'), both(back))]
  transfers between devices with their start and end apart: 5 -> 5, of which waited for: 3 -> 2; matrix products, arithmetic and copies ran while one was open for 11% -> 0% of each run, Pallas kernels for 0% -> 0%
where the time goes in v1:
time: 42.9 us; the launch traced here: 42.6 us
  Pallas kernels  26.9 us (63%)
  starting transfers between devices  12.8 us (30%)
  waiting for transfers between devices  1.92 us (4%)
  local copies, waits for them, and re-layouts  0.83 us (2%)
    pallas_call x1, Pallas kernels, body(): pl.pallas_call(functools.partial(local_kernel, sb), grid=(steps,), in_spe...  17 us
    pallas_call x1, Pallas kernels, body(): pl.pallas_call(functools.partial(finish_kernel, sb, slabs, peers), grid=(...  9.92 us
    ppermute x1, starting transfers between devices, body(): el = lax.ppermute(el, ('slab', 'layer'), both(back))  5.34 us
    ppermute x1, starting transfers between devices, body(): plf = lax.ppermute(plf, 'slab', back)  5.02 us
    ppermute x1, starting transfers between devices, body(): z = lax.ppermute(z, 'layer', [(0, 1), (1, 0)])  1.93 us
    ppermute x1, waiting for transfers between devices, body(): er = lax.ppermute(er, ('slab', 'layer'), both(ring))  1.8 us
  transfers between devices with their start and end apart: 5, of which 2 were waited for; matrix products, arithmetic and copies ran while one was open for 0% of the time, Pallas kernels for 0%

profile of v1, /device:TPU:0, one launch (start us, length us, event | category | flops | bytes accessed | tf_op | source)
XLA Modules:
  0.0 42.6 jit_solution(11055252545485367130)
XLA Ops:
  0.0 17.0 %local.1 = (f32[4096,128]{1,0:T(8,128)}, f32[64,8,128]{2,1,0:T(8,128)}, f32[64,8,128]{2,1,0:T(8,128)}, f32[32,8,128]{2,1,0:T(8,128)}, f32[8,8,128]{2,1,0:T(8,128)}, /*index=5*/f32[8,8,128]{2,1,0:T(8,128)}) custom-call(f32[4096,128]{1,0:T(8,128)} %bitcast.16, f32[12288,128]{1,0:T(8,128)} %bitcast.15, s32[64,1024]{1,0:T(8,128)} %fm_ref.3, ...), custom_call_target="tpu_custom_call" | custom-call | tf_op jit(solution)/shard_map/local/pallas_call | solution.py:272
  17.0 0.6 %collective-permute-start = (f32[64,8,128]{2,1,0:T(8,128)}, f32[64,8,128]{2,1,0:T(8,128)S(1)}, u32[]{:S(2)}, u32[]{:S(2)}) collective-permute-start(f32[64,8,128]{2,1,0:T(8,128)} %get-tuple-element.12), channel_id=1, source_target_pairs={{0,2},{2,4},{4,6},{6,8},{8,10},{10,12},{12,14},{14,16},{16,18},{18... | collective-permute-start | bytes 786440 | tf_op jit(solution)/shard_map/ppermute | solution.py:304
  17.6 5.0 %collective-permute-start.1 = (f32[64,8,128]{2,1,0:T(8,128)}, f32[64,8,128]{2,1,0:T(8,128)S(1)}, u32[]{:S(2)}, u32[]{:S(2)}) collective-permute-start(f32[64,8,128]{2,1,0:T(8,128)} %get-tuple-element.13), channel_id=1, source_target_pairs={{2,0},{4,2},{6,4},{8,6},{10,8},{12,10},{14,12},{16,14},{18,16},{20... | collective-permute-start | bytes 786440 | tf_op jit(solution)/shard_map/ppermute | solution.py:305
  22.6 1.9 %collective-permute-start.2 = (f32[32,8,128]{2,1,0:T(8,128)}, f32[32,8,128]{2,1,0:T(8,128)S(1)}, u32[]{:S(2)}, u32[]{:S(2)}) collective-permute-start(f32[32,8,128]{2,1,0:T(8,128)} %get-tuple-element.14), channel_id=1, source_target_pairs={{0,1},{1,0},{2,3},{3,2},{4,5},{5,4},{6,7},{7,6},{8,9},{9,8},{10,11... | collective-permute-start | bytes 393224 | tf_op jit(solution)/shard_map/ppermute | solution.py:306
  24.5 0.0 collective-permute-start.3
  24.5 5.3 %collective-permute-start.4 = (f32[8,8,128]{2,1,0:T(8,128)}, f32[8,8,128]{2,1,0:T(8,128)S(1)}, u32[]{:S(2)}, u32[]{:S(2)}) collective-permute-start(f32[8,8,128]{2,1,0:T(8,128)} %get-tuple-element.16), channel_id=1, source_target_pairs={{2,1},{3,0},{4,3},{5,2},{6,5},{7,4},{8,7},{9,6},{10,9},{11,8},{12,... | collective-permute-start | bytes 98312 | tf_op jit(solution)/shard_map/ppermute | solution.py:308
  29.9 1.8 %collective-permute-done.3.er_ref = f32[8,8,128]{2,1,0:T(8,128)S(1)} collective-permute-done((f32[8,8,128]{2,1,0:T(8,128)}, f32[8,8,128]{2,1,0:T(8,128)S(1)}, u32[]{:S(2)}, u32[]{:S(2)}) %collective-permute-start.3) | collective-permute-done | bytes 32800 | tf_op jit(solution)/shard_map/ppermute | solution.py:307
  31.7 0.0 copy-start.3
  31.7 0.1 collective-permute-done.4.el_ref
  31.8 0.0 copy-start.4
  31.8 0.0 collective-permute-done.2.z_ref
  31.8 0.0 copy-start.2
  31.8 0.0 collective-permute-done.pr_ref
  31.8 0.0 copy-start
  31.8 0.0 collective-permute-done.1.pl_ref
  31.8 0.0 copy-start.1
  31.8 0.5 %copy-done.3 = f32[8,8,128]{2,1,0:T(8,128)} copy-done((f32[8,8,128]{2,1,0:T(8,128)}, f32[8,8,128]{2,1,0:T(8,128)S(1)}, u32[]{:S(2)}) %copy-start.3) | copy-done | bytes 32792
  32.3 0.1 copy-done.4
  32.4 0.1 copy-done.2
  32.4 0.1 copy-done
  32.6 0.1 copy-done.1
  32.6 9.9 %finish.1 = f32[4096,128]{1,0:T(8,128)} custom-call(s32[1024]{0:T(1024)} %ids_ref.1, f32[4096,128]{1,0:T(8,128)} %get-tuple-element.11.v_ref, s32[64,1024]{1,0:T(8,128)} %fm_ref.3, f32[64,8,128]{2,1,0:T(8,128)} %copy-done, f32[64,8,128]{2,1,0:T(8,128)} %copy-done.1, f32[32,8,128]{2,1,0:T(8,128)} %copy-done.2, f32[8,8,128]{2,1,0:T(8,128)} %copy-done.3, ...), custom_call_target="tpu_custom_call" | custom-call | tf_op jit(solution)/shard_map/finish/pallas_call | solution.py:309
Async XLA Ops:
  17.0 14.8 %collective-permute-start = (f32[64,8,128]{2,1,0:T(8,128)}, f32[64,8,128]{2,1,0:T(8,128)S(1)}, u32[]{:S(2)}, u32[]{:S(2)}) collective-permute-start(f32[64,8,128]{2,1,0:T(8,128)} %get-tuple-element.12), channel_id=1, source_target_pairs={{0,2},{2,4},{4,6},{6,8},{8,10},{10,12},{12,14},{14,16},{16,18},{18... | collective-permute-start | bytes 786440 | tf_op jit(solution)/shard_map/ppermute | solution.py:304
  17.6 14.2 %collective-permute-start.1 = (f32[64,8,128]{2,1,0:T(8,128)}, f32[64,8,128]{2,1,0:T(8,128)S(1)}, u32[]{:S(2)}, u32[]{:S(2)}) collective-permute-start(f32[64,8,128]{2,1,0:T(8,128)} %get-tuple-element.13), channel_id=1, source_target_pairs={{2,0},{4,2},{6,4},{8,6},{10,8},{12,10},{14,12},{16,14},{18,16},{20... | collective-permute-start | bytes 786440 | tf_op jit(solution)/shard_map/ppermute | solution.py:305
  22.6 9.2 %collective-permute-start.2 = (f32[32,8,128]{2,1,0:T(8,128)}, f32[32,8,128]{2,1,0:T(8,128)S(1)}, u32[]{:S(2)}, u32[]{:S(2)}) collective-permute-start(f32[32,8,128]{2,1,0:T(8,128)} %get-tuple-element.14), channel_id=1, source_target_pairs={{0,1},{1,0},{2,3},{3,2},{4,5},{5,4},{6,7},{7,6},{8,9},{9,8},{10,11... | collective-permute-start | bytes 393224 | tf_op jit(solution)/shard_map/ppermute | solution.py:306
  24.5 7.1 %collective-permute-start.3 = (f32[8,8,128]{2,1,0:T(8,128)}, f32[8,8,128]{2,1,0:T(8,128)S(1)}, u32[]{:S(2)}, u32[]{:S(2)}) collective-permute-start(f32[8,8,128]{2,1,0:T(8,128)} %get-tuple-element.15), channel_id=1, source_target_pairs={{0,3},{1,2},{2,5},{3,4},{4,7},{5,6},{6,9},{7,8},{8,11},{9,10},{10,... | collective-permute-start | bytes 98312 | tf_op jit(solution)/shard_map/ppermute | solution.py:307
  24.5 7.3 %collective-permute-start.4 = (f32[8,8,128]{2,1,0:T(8,128)}, f32[8,8,128]{2,1,0:T(8,128)S(1)}, u32[]{:S(2)}, u32[]{:S(2)}) collective-permute-start(f32[8,8,128]{2,1,0:T(8,128)} %get-tuple-element.16), channel_id=1, source_target_pairs={{2,1},{3,0},{4,3},{5,2},{6,5},{7,4},{8,7},{9,6},{10,9},{11,8},{12,... | collective-permute-start | bytes 98312 | tf_op jit(solution)/shard_map/ppermute | solution.py:308
  31.7 0.6 %copy-start.3 = (f32[8,8,128]{2,1,0:T(8,128)}, f32[8,8,128]{2,1,0:T(8,128)S(1)}, u32[]{:S(2)}) copy-start(f32[8,8,128]{2,1,0:T(8,128)S(1)} %collective-permute-done.3.er_ref) | copy-start | bytes 98308
  31.8 0.6 %copy-start.4 = (f32[8,8,128]{2,1,0:T(8,128)}, f32[8,8,128]{2,1,0:T(8,128)S(1)}, u32[]{:S(2)}) copy-start(f32[8,8,128]{2,1,0:T(8,128)S(1)} %collective-permute-done.4.el_ref) | copy-start | bytes 98308
  31.8 0.7 %copy-start.2 = (f32[32,8,128]{2,1,0:T(8,128)}, f32[32,8,128]{2,1,0:T(8,128)S(1)}, u32[]{:S(2)}) copy-start(f32[32,8,128]{2,1,0:T(8,128)S(1)} %collective-permute-done.2.z_ref) | copy-start | bytes 393220
  31.8 0.8 %copy-start = (f32[64,8,128]{2,1,0:T(8,128)}, f32[64,8,128]{2,1,0:T(8,128)S(1)}, u32[]{:S(2)}) copy-start(f32[64,8,128]{2,1,0:T(8,128)S(1)} %collective-permute-done.pr_ref) | copy-start | bytes 786436
  31.8 0.8 %copy-start.1 = (f32[64,8,128]{2,1,0:T(8,128)}, f32[64,8,128]{2,1,0:T(8,128)S(1)}, u32[]{:S(2)}) copy-start(f32[64,8,128]{2,1,0:T(8,128)S(1)} %collective-permute-done.1.pl_ref) | copy-start | bytes 786436

commit v2 on v1

--- a/solution.py
+++ b/solution.py
@@ -191,16 +191,76 @@
     put_faces(4, 0, edges[1])
 
 
-def local_kernel(sb, u_ref, m_ref, fm_ref, fwd_ref, bwd_ref, consts, v_ref, pr_ref, pl_ref, z_ref, er_ref, el_ref):
-    faces = (pr_ref, pl_ref, z_ref, er_ref, el_ref)
+def local_kernel(
+    sb, steps, peers, u_ref, m_ref, fm_ref, fwd_ref, bwd_ref, consts,
+    v_ref, *refs
+):
+    landing, sending, (send_sem, recv_sem) = refs[:5], refs[5:10], refs[10:]
+    step = pl.program_id(0)
+    me, layer = lax.axis_index("slab"), lax.axis_index("layer")
+    right, left = lax.rem(me + 1, peers), lax.rem(me + peers - 1, peers)
+    targets = (
+        {"slab": right, "layer": layer},
+        {"slab": left, "layer": layer},
+        {"slab": me, "layer": 1 - layer},
+        {"slab": right, "layer": 1 - layer},
+        {"slab": left, "layer": 1 - layer},
+    )
+    sizes = (sb, sb, sb // 2, 1, 1)
+    barrier = pltpu.get_barrier_semaphore()
+
+    def copy_of(which, at):
+        rows = pl.ds(at * sizes[which], sizes[which])
+        return pltpu.make_async_remote_copy(
+            src_ref=sending[which].at[rows],
+            dst_ref=landing[which].at[rows],
+            send_sem=send_sem.at[which, at],
+            recv_sem=recv_sem.at[which, at],
+            device_id=targets[which],
+            device_id_type=pl.DeviceIdType.MESH,
+        )
+
+    @pl.when(step == 0)
+    def _():
+        for target in targets:
+            pl.semaphore_signal(
+                barrier, inc=1, device_id=target, device_id_type=pl.DeviceIdType.MESH
+            )
+
+    @pl.when(step == 1)
+    def _():
+        pl.semaphore_wait(barrier, 5)
+
+    @pl.when(step > 0)
+    def _():
+        for which in range(5):
+            copy_of(which, step - 1).start()
 
     def put_v(s, k, value):
         v_ref[pl.ds(s * 64 + k * 8, 8), :] = value
 
     def put_faces(which, at, value):
-        faces[which][at] = value
+        sending[which][step * sizes[which] + at] = value
 
     slab_work(sb, u_ref, m_ref, fm_ref, fwd_ref, bwd_ref, consts, put_v, put_faces)
+
+    @pl.when(step == steps - 1)
+    def _():
+        def drain(at, carry):
+            for which in range(5):
+                copy_of(which, at).wait_send()
+            return carry
+
+        def collect(at, carry):
+            for which in range(5):
+                copy_of(which, at).wait_recv()
+            return carry
+
+        lax.fori_loop(0, steps - 1, drain, 0)
+        for which in range(5):
+            copy_of(which, steps - 1).start()
+        drain(steps - 1, 0)
+        lax.fori_loop(0, steps, collect, 0)
 
 
 def finish_kernel(
@@ -215,8 +275,8 @@
     @pl.when(step == 0)
     def _():
         for p in range(slabs):
-            inv_ref[0, ids_ref[behind + p] // peers] = p
-            inv_ref[1, ids_ref[ahead + p] // peers] = p
+            inv_ref[0, lax.div(ids_ref[behind + p], peers)] = p
+            inv_ref[1, lax.div(ids_ref[ahead + p], peers)] = p
 
     sub, lane = iotas()
     top_mask = (sub >= 4) & (lane >= 64)
@@ -225,15 +285,15 @@
     spread = lane // 8
 
     def edge_of(ref, q):
-        e = pltpu.roll(ref[q // sb], (LANES - 8 * (q % sb)) % LANES, axis=1)
+        e = pltpu.roll(ref[lax.div(q, sb)], LANES - 8 * lax.rem(q, sb), axis=1)
         return jnp.where(
             (sub < 4) & (lane < 8), e, jnp.where((sub >= 4) & (lane >= 120), roll_lane(e, -8), 0.0)
         )
 
     for s in range(sb):
         own = ids_ref[me * slabs + step * sb + s]
-        q_prev = inv_ref[0, lax.rem(own + total - 1, total) // peers]
-        q_next = inv_ref[1, lax.rem(own + 1, total) // peers]
+        q_prev = inv_ref[0, lax.div(lax.rem(own + total - 1, total), peers)]
+        q_next = inv_ref[1, lax.div(lax.rem(own + 1, total), peers)]
         left = pr_ref[q_prev] + edge_of(er_ref, q_prev)
         right = pl_ref[q_next] + edge_of(el_ref, q_next)
         flag = jnp.broadcast_to(fm_ref[s : s + 1, 0:1], (SUB, LANES)) != 0
@@ -270,7 +330,7 @@
     whole = lambda shape: pl.BlockSpec(shape, lambda i: (0,) * len(shape))
     stack = lambda n: pl.BlockSpec((n, SUB, LANES), lambda i: (i, 0, 0))
     v, pr, plf, z, er, el = pl.pallas_call(
-        functools.partial(local_kernel, sb),
+        functools.partial(local_kernel, sb, steps, peers),
         grid=(steps,),
         in_specs=[
             pl.BlockSpec((sb * 64, LANES), lambda i: (i, 0)),
@@ -282,11 +342,7 @@
         ],
         out_specs=[
             pl.BlockSpec((sb * 64, LANES), lambda i: (i, 0)),
-            stack(sb),
-            stack(sb),
-            stack(sb // 2),
-            stack(1),
-            stack(1),
+            *[pl.BlockSpec(memory_space=pl.ANY)] * 5,
         ],
         out_shape=[
             jax.ShapeDtypeStruct((slabs * 64, LANES), f32),
@@ -296,16 +352,18 @@
             jax.ShapeDtypeStruct((steps, SUB, LANES), f32),
             jax.ShapeDtypeStruct((steps, SUB, LANES), f32),
         ],
+        scratch_shapes=[
+            pltpu.VMEM((slabs, SUB, LANES), f32),
+            pltpu.VMEM((slabs, SUB, LANES), f32),
+            pltpu.VMEM((slabs // 2, SUB, LANES), f32),
+            pltpu.VMEM((steps, SUB, LANES), f32),
+            pltpu.VMEM((steps, SUB, LANES), f32),
+            pltpu.SemaphoreType.DMA((5, steps)),
+            pltpu.SemaphoreType.DMA((5, steps)),
+        ],
+        compiler_params=pltpu.CompilerParams(collective_id=0, has_side_effects=True),
         name="local",
     )(u, m, face_map, jnp.asarray(fwd_op), jnp.asarray(bwd_op), jnp.asarray(consts))
-    ring = [(i, (i + 1) % peers) for i in range(peers)]
-    back = [(j, i) for i, j in ring]
-    both = lambda pairs: [(2 * i + l, 2 * j + 1 - l) for i, j in pairs for l in range(2)]
-    pr = lax.ppermute(pr, "slab", ring)
-    plf = lax.ppermute(plf, "slab", back)
-    z = lax.ppermute(z, "layer", [(0, 1), (1, 0)])
-    er = lax.ppermute(er, ("slab", "layer"), both(ring))
-    el = lax.ppermute(el, ("slab", "layer"), both(back))
     out = pl.pallas_call(
         functools.partial(finish_kernel, sb, slabs, peers),
         grid=(steps,),

time: 42.9 us -> 35.7 us (0.83)
  starting transfers between devices: 12.8 us -> 0 us
  Pallas kernels: 26.9 us -> 35.4 us
  waiting for transfers between devices: 1.92 us -> 0 us
  local copies, waits for them, and re-layouts: 0.83 us -> 0 us
    ppermute x5 -> x0, starting transfers between devices: 12.8 us -> none  [the longest x1 5.34 us: body(): el = lax.ppermute(el, ('slab', 'layer'), both(back))]
    pallas_call x1, Pallas kernels: 17 us -> 26.4 us  [body(): pl.pallas_call(functools.partial(local_kernel, sb, steps, peers), grid=(s...]
    ppermute x5 -> x0, waiting for transfers between devices: 1.92 us -> none  [the longest x1 1.8 us: body(): er = lax.ppermute(er, ('slab', 'layer'), both(ring))]
    pallas_call x1, Pallas kernels: 9.92 us -> 9.01 us  [body(): pl.pallas_call(functools.partial(finish_kernel, sb, slabs, peers), grid=(...]
    unnamed x10 -> x0, local copies, waits for them, and re-layouts: 0.83 us -> none
  transfers between devices with their start and end apart: 5 -> 0, of which waited for: 2 -> 0; matrix products, arithmetic and copies ran while one was open for 0% -> 0% of each run, Pallas kernels for 0% -> 0%
where the time goes in v2:
time: 35.7 us; the launch traced here: 35.4 us
  Pallas kernels  35.4 us (99%)
    pallas_call x1, Pallas kernels, body(): pl.pallas_call(functools.partial(local_kernel, sb, steps, peers), grid=(s...  26.4 us
    pallas_call x1, Pallas kernels, body(): pl.pallas_call(functools.partial(finish_kernel, sb, slabs, peers), grid=(...  9.01 us

profile of v2, /device:TPU:0, one launch (start us, length us, event | category | flops | bytes accessed | tf_op | source)
XLA Modules:
  0.0 35.4 jit_solution(11271107395421242345)
XLA Ops:
  0.0 26.4 %local.1 = (f32[4096,128]{1,0:T(8,128)}, f32[64,8,128]{2,1,0:T(8,128)}, f32[64,8,128]{2,1,0:T(8,128)}, f32[32,8,128]{2,1,0:T(8,128)}, f32[8,8,128]{2,1,0:T(8,128)}, /*index=5*/f32[8,8,128]{2,1,0:T(8,128)}) custom-call(f32[4096,128]{1,0:T(8,128)} %bitcast.16, f32[12288,128]{1,0:T(8,128)} %bitcast.15, s32[64,1024]{1,0:T(8,128)} %fm_ref.3, ...), custom_call_target="tpu_custom_call" | custom-call | tf_op jit(solution)/shard_map/local/pallas_call | solution.py:332
  26.4 9.0 %finish.1 = f32[4096,128]{1,0:T(8,128)} custom-call(s32[1024]{0:T(1024)} %ids_ref.1, f32[4096,128]{1,0:T(8,128)} %get-tuple-element.11.v_ref, s32[64,1024]{1,0:T(8,128)} %fm_ref.3, f32[64,8,128]{2,1,0:T(8,128)} %get-tuple-element.12.pr_ref, f32[64,8,128]{2,1,0:T(8,128)} %get-tuple-element.13.pl_ref, f32[32,8,128]{2,1,0:T(8,128)} %get-tuple-element.14.z_ref, ...), custom_call_target="tpu_custom_call" | custom-call | tf_op jit(solution)/shard_map/finish/pallas_call | solution.py:367

commit v3 on v2

--- a/solution.py
+++ b/solution.py
@@ -14,6 +14,8 @@
 EZ = 4
 SUB = 8
 LANES = 128
+SB = 8
+SBF = 16
 
 
 def legendre_pair(nodes, degree):
@@ -72,8 +74,8 @@
             for s in range(2):
                 for l in range(2):
                     c_in = 2 * (2 * li + (l2 ^ s)) + (h ^ l)
-                    zf[lo, li, s, l] = der[c_out, c_in] * rho[c_out] * cube_plane
-                    zb[lo, li, s, l] = der[c_in, c_out]
+                    zf[lo, l, li, s] = np.roll(der[c_out, c_in] * rho[c_out] * cube_plane, 64 * l, 1)
+                    zb[lo, l, li, s] = np.roll(der[c_in, c_out], 64 * l, 1)
     consts = np.concatenate([zf.reshape(-1, SUB, LANES), zb.reshape(-1, SUB, LANES), rc], 0)
     return fwd_op, bwd_op, consts.astype(np.float32)
 
@@ -112,15 +114,19 @@
 def apply_z(pair, consts, base):
     terms = []
     for v in pair:
-        sv = roll_sub(v, 4)
-        terms += [v, roll_lane(v, 64), sv, roll_lane(sv, 64)]
+        terms += [v, roll_sub(v, 4)]
     out = []
     for lo in range(2):
-        acc = consts[base + 8 * lo] * terms[0]
-        for t in range(1, 8):
-            acc = acc + consts[base + 8 * lo + t] * terms[t]
-        out.append(acc)
+        near, far = (
+            sum_of([consts[base + 8 * lo + 4 * half + t] * terms[t] for t in range(4)])
+            for half in range(2)
+        )
+        out.append(near + roll_lane(far, 64))
     return out
+
+
+def sum_of(parts):
+    return (parts[0] + parts[1]) + (parts[2] + parts[3])
 
 
 def slab_work(sb, u_ref, m_ref, fm_ref, fwd_ref, bwd_ref, consts, put_v, put_faces):
@@ -149,8 +155,8 @@
     mask_dn = (ey > 0) & (b == 0)
     top_mask = (sub >= 4) & (lane >= 64)
     bot_mask = (sub < 4) & (lane < 64)
-    group = lane // 16
-    pick = (lane % 16) * 8
+    group = lane // 16 % 4
+    pick = (lane % 16) * 8 + 7 * (lane // 64)
     edges = [None, None]
     z_hold = None
     for s in range(sb):
@@ -168,12 +174,17 @@
             a, c = v[2 * ez + 1], v[2 * ez + 2]
             v[2 * ez + 1] = a + jnp.where(top_mask, roll_lane(roll_sub(c, 4), 64), 0.0)
             v[2 * ez + 2] = c + jnp.where(bot_mask, roll_lane(roll_sub(a, 4), 64), 0.0)
-        left = jnp.zeros((SUB, LANES), jnp.float32)
-        right = left
+        packs = []
         for k in range(8):
             put_v(s, k, v[k])
-            left = jnp.where(group == k, lane_gather(v[k], pick), left)
-            right = jnp.where(group == k, lane_gather(v[k], pick + 7), right)
+            got = lane_gather(v[k], pick)
+            if k % 4 == 0:
+                packs.append(got)
+            else:
+                packs[-1] = jnp.where(group == k % 4, got, packs[-1])
+        low_half = lane < 64
+        left = jnp.where(low_half, packs[0], roll_lane(packs[1], 64))
+        right = jnp.where(low_half, roll_lane(packs[0], 64), packs[1])
         flag = jnp.broadcast_to(fm_ref[s : s + 1, 0:1], (SUB, LANES)) != 0
         right = jnp.where(flag, flip(right, sub, lane), right)
         put_faces(0, s, right)
@@ -264,7 +275,7 @@
 
 
 def finish_kernel(
-    sb, slabs, peers, ids_ref, v_ref, fm_ref, pr_ref, pl_ref, z_ref, er_ref, el_ref, out_ref, inv_ref
+    sb, per_edge, slabs, peers, ids_ref, v_ref, fm_ref, pr_ref, pl_ref, z_ref, er_ref, el_ref, out_ref, inv_ref
 ):
     step = pl.program_id(0)
     me = lax.axis_index("slab")
@@ -282,14 +293,16 @@
     top_mask = (sub >= 4) & (lane >= 64)
     bot_mask = (sub < 4) & (lane < 64)
     a = lane % 8
-    spread = lane // 8
+    on_face = (a == 0) | (a == 7)
+    spread = lane // 8 + 64 * (a == 7).astype(jnp.int32)
 
     def edge_of(ref, q):
-        e = pltpu.roll(ref[lax.div(q, sb)], LANES - 8 * lax.rem(q, sb), axis=1)
+        e = pltpu.roll(ref[lax.div(q, per_edge)], LANES - 8 * lax.rem(q, per_edge), axis=1)
         return jnp.where(
             (sub < 4) & (lane < 8), e, jnp.where((sub >= 4) & (lane >= 120), roll_lane(e, -8), 0.0)
         )
 
+    packs = []
     for s in range(sb):
         own = ids_ref[me * slabs + step * sb + s]
         q_prev = inv_ref[0, lax.div(lax.rem(own + total - 1, total), peers)]
@@ -302,21 +315,26 @@
         if s % 2:
             z = roll_lane(z, 64)
         z = roll_lane(roll_sub(z, 4), 64)
-        for k in range(8):
-            add = jnp.where(
-                a == 0,
-                lane_gather(left, spread + 16 * k),
-                jnp.where(a == 7, lane_gather(right, spread + 16 * k), 0.0),
+        low_half = lane < 64
+        packs.append(
+            (
+                jnp.where(low_half, left, roll_lane(right, 64)),
+                jnp.where(low_half, roll_lane(left, 64), right),
+                z,
             )
-            w = v_ref[pl.ds(s * 64 + k * 8, 8), :] + add
+        )
+    for k in range(8):
+        for s in range(sb):
+            w = v_ref[pl.ds(s * 64 + k * 8, 8), :]
+            w = w + jnp.where(on_face, lane_gather(packs[s][k // 4], spread + 16 * (k % 4)), 0.0)
             if k == 0:
-                w = w + jnp.where(bot_mask, z, 0.0)
+                w = w + jnp.where(bot_mask, packs[s][2], 0.0)
             if k == 7:
-                w = w + jnp.where(top_mask, z, 0.0)
+                w = w + jnp.where(top_mask, packs[s][2], 0.0)
             out_ref[pl.ds(s * 64 + k * 8, 8), :] = w
 
 
-def body(sb, peers, nodal_field, metric, slab_ids, face_map):
+def body(sb, sbf, peers, nodal_field, metric, slab_ids, face_map):
     slabs = nodal_field.shape[1]
     steps = slabs // sb
     fwd_op, bwd_op, consts = tables()
@@ -365,19 +383,19 @@
         name="local",
     )(u, m, face_map, jnp.asarray(fwd_op), jnp.asarray(bwd_op), jnp.asarray(consts))
     out = pl.pallas_call(
-        functools.partial(finish_kernel, sb, slabs, peers),
-        grid=(steps,),
+        functools.partial(finish_kernel, sbf, sb, slabs, peers),
+        grid=(slabs // sbf,),
         in_specs=[
             pl.BlockSpec(memory_space=pltpu.SMEM),
-            pl.BlockSpec((sb * 64, LANES), lambda i: (i, 0)),
-            pl.BlockSpec((sb, LANES), lambda i: (i, 0)),
+            pl.BlockSpec((sbf * 64, LANES), lambda i: (i, 0)),
+            pl.BlockSpec((sbf, LANES), lambda i: (i, 0)),
             whole((slabs, SUB, LANES)),
             whole((slabs, SUB, LANES)),
-            stack(sb // 2),
+            stack(sbf // 2),
             whole((steps, SUB, LANES)),
             whole((steps, SUB, LANES)),
         ],
-        out_specs=pl.BlockSpec((sb * 64, LANES), lambda i: (i, 0)),
+        out_specs=pl.BlockSpec((sbf * 64, LANES), lambda i: (i, 0)),
         out_shape=jax.ShapeDtypeStruct((slabs * 64, LANES), f32),
         scratch_shapes=[pltpu.SMEM((2, slabs), jnp.int32)],
         name="finish",
@@ -388,7 +406,7 @@
 
 def solution(mesh):
     return jax.shard_map(
-        functools.partial(body, 8, mesh.shape["slab"]),
+        functools.partial(body, SB, SBF, mesh.shape["slab"]),
         mesh=mesh,
         in_specs=(
             P("layer", "slab", None, None, None),

time: 35.7 us -> 28.2 us (0.79)
  Pallas kernels: 35.4 us -> 27.9 us
    pallas_call x1, Pallas kernels: 26.4 us -> 21.6 us  [body(): pl.pallas_call(functools.partial(local_kernel, sb, steps, peers), grid=(s...]
    pallas_call x1, Pallas kernels: 9.01 us -> 6.26 us  [body(): pl.pallas_call(functools.partial(finish_kernel, sbf, sb, slabs, peers), g...]
where the time goes in v3:
time: 28.2 us; the launch traced here: 27.9 us
  Pallas kernels  27.9 us (99%)
    pallas_call x1, Pallas kernels, body(): pl.pallas_call(functools.partial(local_kernel, sb, steps, peers), grid=(s...  21.6 us
    pallas_call x1, Pallas kernels, body(): pl.pallas_call(functools.partial(finish_kernel, sbf, sb, slabs, peers), g...  6.26 us

profile of v3, /device:TPU:0, one launch (start us, length us, event | category | flops | bytes accessed | tf_op | source)
XLA Modules:
  0.0 27.9 jit_solution(1208710039257728204)
XLA Ops:
  0.0 21.6 %local.1 = (f32[4096,128]{1,0:T(8,128)}, f32[64,8,128]{2,1,0:T(8,128)}, f32[64,8,128]{2,1,0:T(8,128)}, f32[32,8,128]{2,1,0:T(8,128)}, f32[8,8,128]{2,1,0:T(8,128)}, /*index=5*/f32[8,8,128]{2,1,0:T(8,128)}) custom-call(f32[4096,128]{1,0:T(8,128)} %bitcast.16, f32[12288,128]{1,0:T(8,128)} %bitcast.15, s32[64,1024]{1,0:T(8,128)} %fm_ref.3, ...), custom_call_target="tpu_custom_call" | custom-call | tf_op jit(solution)/shard_map/local/pallas_call | solution.py:350
  21.6 6.3 %finish.1 = f32[4096,128]{1,0:T(8,128)} custom-call(s32[1024]{0:T(1024)} %ids_ref.1, f32[4096,128]{1,0:T(8,128)} %get-tuple-element.11.v_ref, s32[64,1024]{1,0:T(8,128)} %fm_ref.3, f32[64,8,128]{2,1,0:T(8,128)} %get-tuple-element.12.pr_ref, f32[64,8,128]{2,1,0:T(8,128)} %get-tuple-element.13.pl_ref, f32[32,8,128]{2,1,0:T(8,128)} %get-tuple-element.14.z_ref, ...), custom_call_target="tpu_custom_call" | custom-call | tf_op jit(solution)/shard_map/finish/pallas_call | solution.py:385

commit v4 on v3

--- a/solution.py
+++ b/solution.py
@@ -267,9 +267,10 @@
                 copy_of(which, at).wait_recv()
             return carry
 
-        lax.fori_loop(0, steps - 1, drain, 0)
+        lax.fori_loop(0, steps - 2, drain, 0)
         for which in range(5):
             copy_of(which, steps - 1).start()
+        drain(steps - 2, 0)
         drain(steps - 1, 0)
         lax.fori_loop(0, steps, collect, 0)
 

time: 28.2 us -> 28.2 us (level)
  no operation moved by 1% of the time
where the time goes in v4:
time: 28.2 us; the launch traced here: 27.9 us
  Pallas kernels  27.9 us (99%)
    pallas_call x1, Pallas kernels, body(): pl.pallas_call(functools.partial(local_kernel, sb, steps, peers), grid=(s...  21.6 us
    pallas_call x1, Pallas kernels, body(): pl.pallas_call(functools.partial(finish_kernel, sbf, sb, slabs, peers), g...  6.26 us

profile of v4, /device:TPU:0, one launch (start us, length us, event | category | flops | bytes accessed | tf_op | source)
XLA Modules:
  0.0 27.9 jit_solution(1992606493609451441)
XLA Ops:
  0.0 21.6 %local.1 = (f32[4096,128]{1,0:T(8,128)}, f32[64,8,128]{2,1,0:T(8,128)}, f32[64,8,128]{2,1,0:T(8,128)}, f32[32,8,128]{2,1,0:T(8,128)}, f32[8,8,128]{2,1,0:T(8,128)}, /*index=5*/f32[8,8,128]{2,1,0:T(8,128)}) custom-call(f32[4096,128]{1,0:T(8,128)} %bitcast.16, f32[12288,128]{1,0:T(8,128)} %bitcast.15, s32[64,1024]{1,0:T(8,128)} %fm_ref.3, ...), custom_call_target="tpu_custom_call" | custom-call | tf_op jit(solution)/shard_map/local/pallas_call | solution.py:351
  21.6 6.3 %finish.1 = f32[4096,128]{1,0:T(8,128)} custom-call(s32[1024]{0:T(1024)} %ids_ref.1, f32[4096,128]{1,0:T(8,128)} %get-tuple-element.11.v_ref, s32[64,1024]{1,0:T(8,128)} %fm_ref.3, f32[64,8,128]{2,1,0:T(8,128)} %get-tuple-element.12.pr_ref, f32[64,8,128]{2,1,0:T(8,128)} %get-tuple-element.13.pl_ref, f32[32,8,128]{2,1,0:T(8,128)} %get-tuple-element.14.z_ref, ...), custom_call_target="tpu_custom_call" | custom-call | tf_op jit(solution)/shard_map/finish/pallas_call | solution.py:386
